TPU v7x, 32 devices: a whole 2x2x4 slice. The times are simulated.
32 devices in a mesh: row: 8 (over y, x, core), col: 4 (over z).
Axes of the slice: x: 2, y: 2, z: 4, core: 2. Of those that a mesh axis runs over, the one named last changes fastest.
Arguments:
- jacobian: float32 [2, 4096, 256], P(None, ('row', 'col')), may hold values from -0.25 to 0.25
Outputs:
- normal_tiles: float32 [8, 2, 4, 512, 512], P('row', None, 'col')
All inputs are finite; a program needn't handle non-finite values.
Results may differ from a plain program's by a relative error of at most 0.0003.
Values sent between devices are 32-bit elements; how exact they have to be, the bound alone decides.
A program may use at most 64 MiB of HBM per device.

v0:
```python
import jax
import jax.numpy as jnp
from jax import lax
from jax.sharding import PartitionSpec as P


def from_partner(block, axis, distance):
    count = lax.axis_size(axis)
    route = []
    for low in range(count):
        high = low | 1 << distance
        if high != low and high < count:
            route += [(low, high), (high, low)]
    return lax.ppermute(block, axis, route)


def partner_rows(block, bit_number):
    return from_partner(block, ("row", "col"), bit_number)


def body(jacobian):
    row_index = lax.axis_index("row")
    col_index = lax.axis_index("col")
    col_count = lax.axis_size("col")
    cycles = lax.axis_size("row") // col_count
    panel_count = jacobian.shape[0]
    width = jacobian.shape[2]
    own_tile = lax.all_gather(jacobian, "col", axis=1, tiled=True)
    tile_size = own_tile.shape[1]
    col_bits = col_count.bit_length() - 1
    low_row = row_index % col_count
    moved = jacobian
    for bit_number in range(col_bits):
        first = partner_rows(moved, bit_number)
        second = partner_rows(first, bit_number + col_bits)
        differ = low_row >> bit_number & 1 != col_index >> bit_number & 1
        moved = jnp.where(differ, second, moved)
    gathered = lax.all_gather(moved, "row", axis=1, tiled=True)
    gathered = gathered.reshape(panel_count, cycles, tile_size, width)
    partners = [gathered[:, turn_index] for turn_index in range(cycles)]

    def product(partner):
        return jnp.einsum("pak,pbk->ab", own_tile, partner, precision=lax.Precision.HIGHEST)

    def empty_tile(partner):
        return jnp.zeros((tile_size, tile_size), jnp.float32)

    results = []
    for turn_index in range(cycles):
        column_tile = col_index + col_count * turn_index
        results.append(
            lax.cond(column_tile <= row_index, product, empty_tile, partners[turn_index])
        )
    blocks = jnp.stack(results, 0)
    return blocks[None, :, None]


def solution(mesh):
    in_specs = (P(None, ("row", "col"), None),)
    out_specs = P("row", None, "col", None, None)
    return jax.shard_map(body, mesh=mesh, in_specs=in_specs, out_specs=out_specs, check_vma=False)
```

profile of v0, /device:TPU:4, one launch (start us, length us, event | category | flops | bytes accessed | tf_op | source)
XLA Modules:
  0.0 115.7 jit_solution(6772489944896085306)
XLA Ops:
  6.5 0.0 all-gather.3.cloned.1.call-start
  6.5 1.6 %collective-permute-start = (f32[2,128,256]{2,1,0:T(8,128)}, f32[2,128,256]{2,1,0:T(8,128)S(1)}, u32[]{:S(2)}, u32[]{:S(2)}) collective-permute-start(f32[2,128,256]{2,1,0:T(8,128)} %param.5), channel_id=1, source_target_pairs={{0,1},{1,0},{2,3},{3,2},{4,5},{5,4},{6,7},{7,6},{8,9},{9,8},{10,11... | collective-permute-start | bytes 786440 | tf_op jit(solution)/shard_map/ppermute | solution.py:14
  8.1 6.7 %collective-permute-done = f32[2,128,256]{2,1,0:T(8,128)S(1)} collective-permute-done((f32[2,128,256]{2,1,0:T(8,128)}, f32[2,128,256]{2,1,0:T(8,128)S(1)}, u32[]{:S(2)}, u32[]{:S(2)}) %collective-permute-start) | collective-permute-done | bytes 262176 | tf_op jit(solution)/shard_map/ppermute | solution.py:14
  14.8 0.0 collective-permute-start.1
  14.8 1.5 %collective-permute-done.1 = f32[2,128,256]{2,1,0:T(8,128)S(1)} collective-permute-done((f32[2,128,256]{2,1,0:T(8,128)S(1)}, f32[2,128,256]{2,1,0:T(8,128)S(1)}, u32[]{:S(2)}, u32[]{:S(2)}) %collective-permute-start.1) | collective-permute-done | bytes 262176 | tf_op jit(solution)/shard_map/ppermute | solution.py:14
  16.3 1.0 broadcast_select_fusion
  17.3 2.7 %collective-permute-start.2 = (f32[2,128,256]{2,1,0:T(8,128)S(1)}, f32[2,128,256]{2,1,0:T(8,128)S(1)}, u32[]{:S(2)}, u32[]{:S(2)}) collective-permute-start(f32[2,128,256]{2,1,0:T(8,128)S(1)} %broadcast_select_fusion), channel_id=1, source_target_pairs={{0,2},{2,0},{1,3},{3,1},{4,6},{6,4},{5,7},{7,5},{8,10},{10,8},{9,1... | collective-permute-start | bytes 786440 | tf_op jit(solution)/shard_map/ppermute | solution.py:14
  20.0 11.3 %collective-permute-done.2 = f32[2,128,256]{2,1,0:T(8,128)S(1)} collective-permute-done((f32[2,128,256]{2,1,0:T(8,128)S(1)}, f32[2,128,256]{2,1,0:T(8,128)S(1)}, u32[]{:S(2)}, u32[]{:S(2)}) %collective-permute-start.2) | collective-permute-done | bytes 262176 | tf_op jit(solution)/shard_map/ppermute | solution.py:14
  31.3 1.5 %collective-permute-start.3 = (f32[2,128,256]{2,1,0:T(8,128)S(1)}, f32[2,128,256]{2,1,0:T(8,128)S(1)}, u32[]{:S(2)}, u32[]{:S(2)}) collective-permute-start(f32[2,128,256]{2,1,0:T(8,128)S(1)} %collective-permute-done.2), channel_id=1, source_target_pairs={{0,8},{8,0},{1,9},{9,1},{2,10},{10,2},{3,11},{11,3},{4,12},{12,4},... | collective-permute-start | bytes 786440 | tf_op jit(solution)/shard_map/ppermute | solution.py:14
  32.8 5.1 %collective-permute-done.3 = f32[2,128,256]{2,1,0:T(8,128)S(1)} collective-permute-done((f32[2,128,256]{2,1,0:T(8,128)S(1)}, f32[2,128,256]{2,1,0:T(8,128)S(1)}, u32[]{:S(2)}, u32[]{:S(2)}) %collective-permute-start.3) | collective-permute-done | bytes 262176 | tf_op jit(solution)/shard_map/ppermute | solution.py:14
  37.8 0.7 broadcast_select_fusion.1
  38.6 0.0 all-gather.3.cloned.1.call-update
  38.6 0.0 all-gather.5.cloned.1.call-start
  38.7 0.7 all-gather.5.cloned.1.call-update
  39.4 30.0 %all-gather.3.cloned.1.call-done = f32[2,1024,256]{2,1,0:T(8,128)} async-done(((f32[2,128,256]{2,1,0:T(8,128)}), f32[2,1024,256]{2,1,0:T(8,128)}) %all-gather.3.cloned.1.call-update) | async-done | bytes 2097168 | tf_op jit(solution)/shard_map/all_gather | solution.py:38
  69.3 1.7 %copy.2 = f32[2,2,512,256]{3,2,0,1:T(8,128)S(1)} copy(f32[2,2,512,256]{3,2,1,0:T(8,128)} %bitcast.17) | data formatting | bytes 4194304 | tf_op jit(solution)/shard_map/cond | solution.py:52
  71.1 27.9 %all-gather.5.cloned.1.call-done = f32[2,512,256]{2,1,0:T(8,128)} async-done(((f32[2,128,256]{2,1,0:T(8,128)}), f32[2,512,256]{2,1,0:T(8,128)}) %all-gather.5.cloned.1.call-update) | async-done | bytes 1048592 | tf_op jit(solution)/shard_map/all_gather | solution.py:28
  99.0 3.1 %conditional.3 = (f32[1,512,512]{2,1,0:T(8,128)S(1)}) conditional(s32[]{:T(128)} %convert_element_type.7, () %tuple.23, (f32[2,2,512,256]{3,2,0,1:T(8,128)S(1)}, f32[2,512,256]{2,1,0:T(8,128)}) %tuple.24), branch_computations={%region_2.3_spmd, %region_3.4_spmd} | conditional | flops 1610612736 | bytes 3145736 | solution.py:52
  99.0 3.1 %convolution_bitcast_fusion.1 = f32[1,512,512]{2,1,0:T(8,128)S(1)} fusion(f32[2,512,256]{2,1,0:T(8,128)} %get-tuple-element.27, f32[2,2,512,256]{3,2,0,1:T(8,128)S(1)} %get-tuple-element.28), kind=kOutput, calls=%fused_computation.3 | convolution fusion | flops 1610612736 | bytes 3145728 | tf_op jit(solution)/shard_map/cond/branch_1_fun/pak,pbk->ab/dot_general | solution.py:43
  102.1 4.1 %conditional.2 = (f32[1,512,512]{2,1,0:T(8,128)}) conditional(s32[]{:T(128)} %convert_element_type.6, () %tuple.21, (f32[2,2,512,256]{3,2,0,1:T(8,128)S(1)}, f32[2,512,256]{2,1,0:T(8,128)}) %tuple.24), branch_computations={%region_0.1_spmd, %region_1.2_spmd} | conditional | flops 1610612736 | bytes 3145736 | solution.py:52
  102.1 4.1 %convolution_bitcast_fusion = f32[1,512,512]{2,1,0:T(8,128)} fusion(f32[2,512,256]{2,1,0:T(8,128)} %get-tuple-element.25, f32[2,2,512,256]{3,2,0,1:T(8,128)S(1)} %get-tuple-element.26), kind=kOutput, calls=%fused_computation | convolution fusion | flops 1610612736 | bytes 3145728 | tf_op jit(solution)/shard_map/cond/branch_1_fun/pak,pbk->ab/dot_general | solution.py:43
  106.2 2.7 %maximum_bitcast_fusion = f32[1,2,1,512,512]{4,3,2,1,0:T(8,128)} fusion(f32[1,512,512]{2,1,0:T(8,128)S(1)} %get-tuple-element.34, f32[1,512,512]{2,1,0:T(8,128)} %get-tuple-element.33), kind=kLoop, calls=%fused_computation.6 | loop fusion | flops 524288 | bytes 4194304 | tf_op jit(solution)/shard_map/broadcast_in_dim | solution.py:55
Async XLA Ops:
  6.5 62.8 %all-gather.3.cloned.1.call-start = ((), (), s32[]{:S(2)}) async-start(), calls=%async_computation | async-start | bytes 2359296 | tf_op jit(solution)/shard_map/all_gather | solution.py:38
  6.5 8.3 %collective-permute-start = (f32[2,128,256]{2,1,0:T(8,128)}, f32[2,128,256]{2,1,0:T(8,128)S(1)}, u32[]{:S(2)}, u32[]{:S(2)}) collective-permute-start(f32[2,128,256]{2,1,0:T(8,128)} %param.5), channel_id=1, source_target_pairs={{0,1},{1,0},{2,3},{3,2},{4,5},{5,4},{6,7},{7,6},{8,9},{9,8},{10,11... | collective-permute-start | bytes 786440 | tf_op jit(solution)/shard_map/ppermute | solution.py:14
  14.8 1.5 %collective-permute-start.1 = (f32[2,128,256]{2,1,0:T(8,128)S(1)}, f32[2,128,256]{2,1,0:T(8,128)S(1)}, u32[]{:S(2)}, u32[]{:S(2)}) collective-permute-start(f32[2,128,256]{2,1,0:T(8,128)S(1)} %collective-permute-done), channel_id=1, source_target_pairs={{0,4},{4,0},{1,5},{5,1},{2,6},{6,2},{3,7},{7,3},{8,12},{12,8},{9,1... | collective-permute-start | bytes 786440 | tf_op jit(solution)/shard_map/ppermute | solution.py:14
  17.3 14.0 %collective-permute-start.2 = (f32[2,128,256]{2,1,0:T(8,128)S(1)}, f32[2,128,256]{2,1,0:T(8,128)S(1)}, u32[]{:S(2)}, u32[]{:S(2)}) collective-permute-start(f32[2,128,256]{2,1,0:T(8,128)S(1)} %broadcast_select_fusion), channel_id=1, source_target_pairs={{0,2},{2,0},{1,3},{3,1},{4,6},{6,4},{5,7},{7,5},{8,10},{10,8},{9,1... | collective-permute-start | bytes 786440 | tf_op jit(solution)/shard_map/ppermute | solution.py:14
  31.3 6.5 %collective-permute-start.3 = (f32[2,128,256]{2,1,0:T(8,128)S(1)}, f32[2,128,256]{2,1,0:T(8,128)S(1)}, u32[]{:S(2)}, u32[]{:S(2)}) collective-permute-start(f32[2,128,256]{2,1,0:T(8,128)S(1)} %collective-permute-done.2), channel_id=1, source_target_pairs={{0,8},{8,0},{1,9},{9,1},{2,10},{10,2},{3,11},{11,3},{4,12},{12,4},... | collective-permute-start | bytes 786440 | tf_op jit(solution)/shard_map/ppermute | solution.py:14
  38.6 60.4 %all-gather.5.cloned.1.call-start = ((), (), s32[]{:S(2)}) async-start(), calls=%async_computation.1 | async-start | bytes 1310720 | tf_op jit(solution)/shard_map/all_gather | solution.py:28
Sparse Core Ops, SparseCore 0:
  38.7 30.5 all-gather.2
  70.9 28.0 all-gather.4
where the time goes:
time: 116 us
  waiting for transfers between devices  83.2 us (72%)
  between operations  13.4 us (12%)
  matrix products  7.14 us (6%)
  starting transfers between devices  5.77 us (5%)
  other arithmetic  4.43 us (4%)
  local copies, waits for them, and re-layouts  1.73 us (1%)
    all_gather x1, waiting for transfers between devices, body(): gathered = lax.all_gather(moved, 'row', axis=1, tiled=True)  30 us
    all_gather x1, waiting for transfers between devices, body(): own_tile = lax.all_gather(jacobian, 'col', axis=1, tiled=True)  27.9 us
    ppermute x4, waiting for transfers between devices, from_partner(): return lax.ppermute(block, axis, route)  24.6 us
    dot_general x2, matrix products, product(): jnp.einsum('pak,pbk->ab', own_tile, partner, precision=lax.Precision.HIGH...  7.14 us
    ppermute x4, starting transfers between devices, from_partner(): return lax.ppermute(block, axis, route)  5.72 us
    broadcast_in_dim x1, other arithmetic, body(): return blocks[None, :, None]  2.71 us
  transfers between devices with their start and end apart: 6, of which 6 were waited for; matrix products, arithmetic and copies ran while one was open for 1% of the time, Pallas kernels for 0%

commit v1 on v0

--- a/solution.py
+++ b/solution.py
@@ -35,7 +35,12 @@
         second = partner_rows(first, bit_number + col_bits)
         differ = low_row >> bit_number & 1 != col_index >> bit_number & 1
         moved = jnp.where(differ, second, moved)
-    gathered = lax.all_gather(moved, "row", axis=1, tiled=True)
+    ring = [moved]
+    for hop in range(7):
+        ring.append(lax.ppermute(ring[-1], "row", [(dev, (dev + 1) % 8) for dev in range(8)]))
+    gathered = jnp.roll(
+        jnp.concatenate(ring[::-1], axis=1), (lax.axis_index("row") + 1) * ring[0].shape[1], axis=1
+    )
     gathered = gathered.reshape(panel_count, cycles, tile_size, width)
     partners = [gathered[:, turn_index] for turn_index in range(cycles)]
 

time: 116 us -> 126 us (1.086)
  waiting for transfers between devices: 83.2 us -> 95.3 us
    ppermute x0 -> x7, waiting for transfers between devices: none -> 46.8 us  [body(): lax.ppermute(ring[-1], 'row', [(dev, (dev + 1) % 8) for dev in range(8)])]
    all_gather x1 -> x0, waiting for transfers between devices: 30 us -> none  [body(): gathered = lax.all_gather(moved, 'row', axis=1, tiled=True)]
    all_gather x1, waiting for transfers between devices: 27.9 us -> 23.9 us  [body(): own_tile = lax.all_gather(jacobian, 'col', axis=1, tiled=True)]
    cond x1, local copies, waits for them, and re-layouts: 1.73 us -> 0.14 us  [body(): lax.cond(column_tile <= row_index, product, empty_tile, partners[turn_ind...]
  transfers between devices with their start and end apart: 6 -> 12, of which waited for: 6 -> 12; matrix products, arithmetic and copies ran while one was open for 1% -> 0% of each run, Pallas kernels for 0% -> 0%
where the time goes in v1:
time: 126 us
  waiting for transfers between devices  95.3 us (76%)
  between operations  13.6 us (11%)
  matrix products  7.15 us (6%)
  starting transfers between devices  5.8 us (5%)
  other arithmetic  3.73 us (3%)
    ppermute x7, waiting for transfers between devices, body(): lax.ppermute(ring[-1], 'row', [(dev, (dev + 1) % 8) for dev in range(8)])  46.8 us
    ppermute x4, waiting for transfers between devices, from_partner(): return lax.ppermute(block, axis, route)  24.6 us
    all_gather x1, waiting for transfers between devices, body(): own_tile = lax.all_gather(jacobian, 'col', axis=1, tiled=True)  23.9 us
    dot_general x2, matrix products, product(): jnp.einsum('pak,pbk->ab', own_tile, partner, precision=lax.Precision.HIGH...  7.15 us
    ppermute x4, starting transfers between devices, from_partner(): return lax.ppermute(block, axis, route)  5.72 us
    broadcast_in_dim x1, other arithmetic, body(): return blocks[None, :, None]  2.71 us
  transfers between devices with their start and end apart: 12, of which 12 were waited for; matrix products, arithmetic and copies ran while one was open for 0% of the time, Pallas kernels for 0%

profile of v1, /device:TPU:4, one launch (start us, length us, event | category | flops | bytes accessed | tf_op | source)
XLA Modules:
  0.0 126.2 jit_solution(11866108046878001216)
XLA Ops:
  6.5 0.0 all-gather.2.cloned.1.call-start
  6.5 1.6 %collective-permute-start = (f32[2,128,256]{2,1,0:T(8,128)}, f32[2,128,256]{2,1,0:T(8,128)S(1)}, u32[]{:S(2)}, u32[]{:S(2)}) collective-permute-start(f32[2,128,256]{2,1,0:T(8,128)} %param.5), channel_id=1, source_target_pairs={{0,1},{1,0},{2,3},{3,2},{4,5},{5,4},{6,7},{7,6},{8,9},{9,8},{10,11... | collective-permute-start | bytes 786440 | tf_op jit(solution)/shard_map/ppermute | solution.py:14
  8.1 6.7 %collective-permute-done = f32[2,128,256]{2,1,0:T(8,128)S(1)} collective-permute-done((f32[2,128,256]{2,1,0:T(8,128)}, f32[2,128,256]{2,1,0:T(8,128)S(1)}, u32[]{:S(2)}, u32[]{:S(2)}) %collective-permute-start) | collective-permute-done | bytes 262176 | tf_op jit(solution)/shard_map/ppermute | solution.py:14
  14.8 0.0 collective-permute-start.1
  14.8 1.5 %collective-permute-done.1 = f32[2,128,256]{2,1,0:T(8,128)S(1)} collective-permute-done((f32[2,128,256]{2,1,0:T(8,128)S(1)}, f32[2,128,256]{2,1,0:T(8,128)S(1)}, u32[]{:S(2)}, u32[]{:S(2)}) %collective-permute-start.1) | collective-permute-done | bytes 262176 | tf_op jit(solution)/shard_map/ppermute | solution.py:14
  16.3 1.0 broadcast_select_fusion
  17.3 2.7 %collective-permute-start.2 = (f32[2,128,256]{2,1,0:T(8,128)S(1)}, f32[2,128,256]{2,1,0:T(8,128)S(1)}, u32[]{:S(2)}, u32[]{:S(2)}) collective-permute-start(f32[2,128,256]{2,1,0:T(8,128)S(1)} %broadcast_select_fusion), channel_id=1, source_target_pairs={{0,2},{2,0},{1,3},{3,1},{4,6},{6,4},{5,7},{7,5},{8,10},{10,8},{9,1... | collective-permute-start | bytes 786440 | tf_op jit(solution)/shard_map/ppermute | solution.py:14
  20.0 11.3 %collective-permute-done.2 = f32[2,128,256]{2,1,0:T(8,128)S(1)} collective-permute-done((f32[2,128,256]{2,1,0:T(8,128)S(1)}, f32[2,128,256]{2,1,0:T(8,128)S(1)}, u32[]{:S(2)}, u32[]{:S(2)}) %collective-permute-start.2) | collective-permute-done | bytes 262176 | tf_op jit(solution)/shard_map/ppermute | solution.py:14
  31.3 1.5 %collective-permute-start.3 = (f32[2,128,256]{2,1,0:T(8,128)S(1)}, f32[2,128,256]{2,1,0:T(8,128)S(1)}, u32[]{:S(2)}, u32[]{:S(2)}) collective-permute-start(f32[2,128,256]{2,1,0:T(8,128)S(1)} %collective-permute-done.2), channel_id=1, source_target_pairs={{0,8},{8,0},{1,9},{9,1},{2,10},{10,2},{3,11},{11,3},{4,12},{12,4},... | collective-permute-start | bytes 786440 | tf_op jit(solution)/shard_map/ppermute | solution.py:14
  32.8 5.1 %collective-permute-done.3 = f32[2,128,256]{2,1,0:T(8,128)S(1)} collective-permute-done((f32[2,128,256]{2,1,0:T(8,128)S(1)}, f32[2,128,256]{2,1,0:T(8,128)S(1)}, u32[]{:S(2)}, u32[]{:S(2)}) %collective-permute-start.3) | collective-permute-done | bytes 262176 | tf_op jit(solution)/shard_map/ppermute | solution.py:14
  37.9 0.1 collective-permute-start.4
  37.9 6.7 %collective-permute-done.4 = f32[2,128,256]{2,1,0:T(8,128)S(1)} collective-permute-done((f32[2,128,256]{2,1,0:T(8,128)S(1)}, f32[2,128,256]{2,1,0:T(8,128)S(1)}, u32[]{:S(2)}, u32[]{:S(2)}) %collective-permute-start.4) | collective-permute-done | bytes 262176 | tf_op jit(solution)/shard_map/ppermute | solution.py:40
  44.6 0.0 collective-permute-start.5
  44.6 6.7 %collective-permute-done.5 = f32[2,128,256]{2,1,0:T(8,128)S(1)} collective-permute-done((f32[2,128,256]{2,1,0:T(8,128)S(1)}, f32[2,128,256]{2,1,0:T(8,128)S(1)}, u32[]{:S(2)}, u32[]{:S(2)}) %collective-permute-start.5) | collective-permute-done | bytes 262176 | tf_op jit(solution)/shard_map/ppermute | solution.py:40
  51.3 0.0 collective-permute-start.6
  51.3 6.7 %collective-permute-done.6 = f32[2,128,256]{2,1,0:T(8,128)S(1)} collective-permute-done((f32[2,128,256]{2,1,0:T(8,128)S(1)}, f32[2,128,256]{2,1,0:T(8,128)S(1)}, u32[]{:S(2)}, u32[]{:S(2)}) %collective-permute-start.6) | collective-permute-done | bytes 262176 | tf_op jit(solution)/shard_map/ppermute | solution.py:40
  58.0 0.0 collective-permute-start.7
  58.0 6.7 %collective-permute-done.7 = f32[2,128,256]{2,1,0:T(8,128)S(1)} collective-permute-done((f32[2,128,256]{2,1,0:T(8,128)S(1)}, f32[2,128,256]{2,1,0:T(8,128)S(1)}, u32[]{:S(2)}, u32[]{:S(2)}) %collective-permute-start.7) | collective-permute-done | bytes 262176 | tf_op jit(solution)/shard_map/ppermute | solution.py:40
  64.7 0.0 collective-permute-start.8
  64.7 6.7 %collective-permute-done.8 = f32[2,128,256]{2,1,0:T(8,128)S(1)} collective-permute-done((f32[2,128,256]{2,1,0:T(8,128)S(1)}, f32[2,128,256]{2,1,0:T(8,128)S(1)}, u32[]{:S(2)}, u32[]{:S(2)}) %collective-permute-start.8) | collective-permute-done | bytes 262176 | tf_op jit(solution)/shard_map/ppermute | solution.py:40
  71.4 0.0 collective-permute-start.9
  71.4 6.7 %collective-permute-done.9 = f32[2,128,256]{2,1,0:T(8,128)S(1)} collective-permute-done((f32[2,128,256]{2,1,0:T(8,128)S(1)}, f32[2,128,256]{2,1,0:T(8,128)S(1)}, u32[]{:S(2)}, u32[]{:S(2)}) %collective-permute-start.9) | collective-permute-done | bytes 262176 | tf_op jit(solution)/shard_map/ppermute | solution.py:40
  78.1 0.0 collective-permute-start.10
  78.1 0.0 all-gather.2.cloned.1.call-update
  78.2 6.6 %collective-permute-done.10 = f32[2,128,256]{2,1,0:T(8,128)S(1)} collective-permute-done((f32[2,128,256]{2,1,0:T(8,128)S(1)}, f32[2,128,256]{2,1,0:T(8,128)S(1)}, u32[]{:S(2)}, u32[]{:S(2)}) %collective-permute-start.10) | collective-permute-done | bytes 262176 | tf_op jit(solution)/shard_map/ppermute | solution.py:40
  85.3 0.1 constant_dynamic-slice_fusion
  85.4 0.1 copy.2
  85.5 23.9 %all-gather.2.cloned.1.call-done = f32[2,512,256]{2,1,0:T(8,128)} async-done(((f32[2,128,256]{2,1,0:T(8,128)}), f32[2,512,256]{2,1,0:T(8,128)}) %all-gather.2.cloned.1.call-update) | async-done | bytes 1048592 | tf_op jit(solution)/shard_map/all_gather | solution.py:28
  109.4 3.1 %conditional.2 = (f32[1,512,512]{2,1,0:T(8,128)S(1)}) conditional(s32[]{:T(128)} %convert_element_type.6, () %tuple.21, (f32[2,2,512,256]{3,2,0,1:T(8,128)S(1)}, f32[2,512,256]{2,1,0:T(8,128)}) %tuple.24), branch_computations={%region_0.1_spmd, %region_1.2_spmd} | conditional | flops 1610612736 | bytes 3145736 | solution.py:57
  109.4 3.1 %convolution_bitcast_fusion = f32[1,512,512]{2,1,0:T(8,128)S(1)} fusion(f32[2,512,256]{2,1,0:T(8,128)} %get-tuple-element.25, f32[2,2,512,256]{3,2,0,1:T(8,128)S(1)} %get-tuple-element.26), kind=kOutput, calls=%fused_computation | convolution fusion | flops 1610612736 | bytes 3145728 | tf_op jit(solution)/shard_map/cond/branch_1_fun/pak,pbk->ab/dot_general | solution.py:48
  112.5 4.1 %conditional.3 = (f32[1,512,512]{2,1,0:T(8,128)}) conditional(s32[]{:T(128)} %convert_element_type.7, () %tuple.23, (f32[2,2,512,256]{3,2,0,1:T(8,128)S(1)}, f32[2,512,256]{2,1,0:T(8,128)}) %tuple.24), branch_computations={%region_2.3_spmd, %region_3.4_spmd} | conditional | flops 1610612736 | bytes 3145736 | solution.py:57
  112.5 4.1 %convolution_bitcast_fusion.1 = f32[1,512,512]{2,1,0:T(8,128)} fusion(f32[2,512,256]{2,1,0:T(8,128)} %get-tuple-element.27, f32[2,2,512,256]{3,2,0,1:T(8,128)S(1)} %get-tuple-element.28), kind=kOutput, calls=%fused_computation.3 | convolution fusion | flops 1610612736 | bytes 3145728 | tf_op jit(solution)/shard_map/cond/branch_1_fun/pak,pbk->ab/dot_general | solution.py:48
  116.6 2.7 %maximum_bitcast_fusion = f32[1,2,1,512,512]{4,3,2,1,0:T(8,128)} fusion(f32[1,512,512]{2,1,0:T(8,128)} %get-tuple-element.34, f32[1,512,512]{2,1,0:T(8,128)S(1)} %get-tuple-element.33), kind=kLoop, calls=%fused_computation.6 | loop fusion | flops 524288 | bytes 4194304 | tf_op jit(solution)/shard_map/broadcast_in_dim | solution.py:60
  (17 shorter events, 0.4 us)
Async XLA Ops:
  6.5 102.9 %all-gather.2.cloned.1.call-start = ((), (), s32[]{:S(2)}) async-start(), calls=%async_computation | async-start | bytes 1310720 | tf_op jit(solution)/shard_map/all_gather | solution.py:28
  6.5 8.3 %collective-permute-start = (f32[2,128,256]{2,1,0:T(8,128)}, f32[2,128,256]{2,1,0:T(8,128)S(1)}, u32[]{:S(2)}, u32[]{:S(2)}) collective-permute-start(f32[2,128,256]{2,1,0:T(8,128)} %param.5), channel_id=1, source_target_pairs={{0,1},{1,0},{2,3},{3,2},{4,5},{5,4},{6,7},{7,6},{8,9},{9,8},{10,11... | collective-permute-start | bytes 786440 | tf_op jit(solution)/shard_map/ppermute | solution.py:14
  14.8 1.5 %collective-permute-start.1 = (f32[2,128,256]{2,1,0:T(8,128)S(1)}, f32[2,128,256]{2,1,0:T(8,128)S(1)}, u32[]{:S(2)}, u32[]{:S(2)}) collective-permute-start(f32[2,128,256]{2,1,0:T(8,128)S(1)} %collective-permute-done), channel_id=1, source_target_pairs={{0,4},{4,0},{1,5},{5,1},{2,6},{6,2},{3,7},{7,3},{8,12},{12,8},{9,1... | collective-permute-start | bytes 786440 | tf_op jit(solution)/shard_map/ppermute | solution.py:14
  17.3 14.0 %collective-permute-start.2 = (f32[2,128,256]{2,1,0:T(8,128)S(1)}, f32[2,128,256]{2,1,0:T(8,128)S(1)}, u32[]{:S(2)}, u32[]{:S(2)}) collective-permute-start(f32[2,128,256]{2,1,0:T(8,128)S(1)} %broadcast_select_fusion), channel_id=1, source_target_pairs={{0,2},{2,0},{1,3},{3,1},{4,6},{6,4},{5,7},{7,5},{8,10},{10,8},{9,1... | collective-permute-start | bytes 786440 | tf_op jit(solution)/shard_map/ppermute | solution.py:14
  31.3 6.5 %collective-permute-start.3 = (f32[2,128,256]{2,1,0:T(8,128)S(1)}, f32[2,128,256]{2,1,0:T(8,128)S(1)}, u32[]{:S(2)}, u32[]{:S(2)}) collective-permute-start(f32[2,128,256]{2,1,0:T(8,128)S(1)} %collective-permute-done.2), channel_id=1, source_target_pairs={{0,8},{8,0},{1,9},{9,1},{2,10},{10,2},{3,11},{11,3},{4,12},{12,4},... | collective-permute-start | bytes 786440 | tf_op jit(solution)/shard_map/ppermute | solution.py:14
  37.9 6.7 %collective-permute-start.4 = (f32[2,128,256]{2,1,0:T(8,128)S(1)}, f32[2,128,256]{2,1,0:T(8,128)S(1)}, u32[]{:S(2)}, u32[]{:S(2)}) collective-permute-start(f32[2,128,256]{2,1,0:T(8,128)S(1)} %broadcast_select_fusion.1), channel_id=1, source_target_pairs={{0,4},{4,8},{8,12},{12,16},{16,20},{20,24},{24,28},{28,0},{1,5},{5... | collective-permute-start | bytes 786440 | tf_op jit(solution)/shard_map/ppermute | solution.py:40
  44.6 6.7 %collective-permute-start.5 = (f32[2,128,256]{2,1,0:T(8,128)S(1)}, f32[2,128,256]{2,1,0:T(8,128)S(1)}, u32[]{:S(2)}, u32[]{:S(2)}) collective-permute-start(f32[2,128,256]{2,1,0:T(8,128)S(1)} %collective-permute-done.4), channel_id=1, source_target_pairs={{0,4},{4,8},{8,12},{12,16},{16,20},{20,24},{24,28},{28,0},{1,5},{5... | collective-permute-start | bytes 786440 | tf_op jit(solution)/shard_map/ppermute | solution.py:40
  51.3 6.7 %collective-permute-start.6 = (f32[2,128,256]{2,1,0:T(8,128)S(1)}, f32[2,128,256]{2,1,0:T(8,128)S(1)}, u32[]{:S(2)}, u32[]{:S(2)}) collective-permute-start(f32[2,128,256]{2,1,0:T(8,128)S(1)} %collective-permute-done.5), channel_id=1, source_target_pairs={{0,4},{4,8},{8,12},{12,16},{16,20},{20,24},{24,28},{28,0},{1,5},{5... | collective-permute-start | bytes 786440 | tf_op jit(solution)/shard_map/ppermute | solution.py:40
  58.0 6.7 %collective-permute-start.7 = (f32[2,128,256]{2,1,0:T(8,128)S(1)}, f32[2,128,256]{2,1,0:T(8,128)S(1)}, u32[]{:S(2)}, u32[]{:S(2)}) collective-permute-start(f32[2,128,256]{2,1,0:T(8,128)S(1)} %collective-permute-done.6), channel_id=1, source_target_pairs={{0,4},{4,8},{8,12},{12,16},{16,20},{20,24},{24,28},{28,0},{1,5},{5... | collective-permute-start | bytes 786440 | tf_op jit(solution)/shard_map/ppermute | solution.py:40
  64.7 6.7 %collective-permute-start.8 = (f32[2,128,256]{2,1,0:T(8,128)S(1)}, f32[2,128,256]{2,1,0:T(8,128)S(1)}, u32[]{:S(2)}, u32[]{:S(2)}) collective-permute-start(f32[2,128,256]{2,1,0:T(8,128)S(1)} %collective-permute-done.7), channel_id=1, source_target_pairs={{0,4},{4,8},{8,12},{12,16},{16,20},{20,24},{24,28},{28,0},{1,5},{5... | collective-permute-start | bytes 786440 | tf_op jit(solution)/shard_map/ppermute | solution.py:40
  71.4 6.7 %collective-permute-start.9 = (f32[2,128,256]{2,1,0:T(8,128)S(1)}, f32[2,128,256]{2,1,0:T(8,128)S(1)}, u32[]{:S(2)}, u32[]{:S(2)}) collective-permute-start(f32[2,128,256]{2,1,0:T(8,128)S(1)} %collective-permute-done.8), channel_id=1, source_target_pairs={{0,4},{4,8},{8,12},{12,16},{16,20},{20,24},{24,28},{28,0},{1,5},{5... | collective-permute-start | bytes 786440 | tf_op jit(solution)/shard_map/ppermute | solution.py:40
  78.1 6.7 %collective-permute-start.10 = (f32[2,128,256]{2,1,0:T(8,128)S(1)}, f32[2,128,256]{2,1,0:T(8,128)S(1)}, u32[]{:S(2)}, u32[]{:S(2)}) collective-permute-start(f32[2,128,256]{2,1,0:T(8,128)S(1)} %collective-permute-done.9), channel_id=1, source_target_pairs={{0,4},{4,8},{8,12},{12,16},{16,20},{20,24},{24,28},{28,0},{1,5},{5... | collective-permute-start | bytes 786440 | tf_op jit(solution)/shard_map/ppermute | solution.py:40
Sparse Core Ops, SparseCore 0:
  78.3 31.1 all-gather.1
